TPU v7x, 32 devices: a whole 2x2x4 slice. The times are simulated.
32 devices in a mesh: row: 4 (over x, core), col: 4 (over z), depth: 2 (over y).
Axes of the slice: x: 2, y: 2, z: 4, core: 2. Of those that a mesh axis runs over, the one named last changes fastest.
Arguments:
- trailing: float32 [3008, 48128], P('depth', ('row', 'col')), may hold values from -6 to 6
- panel_block: float32 [48128, 1024], P(('row', 'col', 'depth')), may hold values from -6 to 6
- factor_panel: float32 [48128, 1024], P(('row', 'col', 'depth')), may hold values from -0.1875 to 0.1875
- corner_block: float32 [1024, 1024], P(('row', 'col', 'depth')), may hold values from -6 to 6, as said below
- corner_inverse: float32 [1024, 1024], P(('row', 'col', 'depth')), may hold values from -1 to 2, as said below
Outputs:
- trailing_out: float32 [3008, 48128], P('depth', ('row', 'col'))
- panel_out: float32 [48128, 1024], P(('row', 'col', 'depth'))
- corner_out: float32 [1024, 1024], P(('row', 'col', 'depth'))
Inputs may be any that keep to these rules, and one draw needn't show every extreme that they name: `corner_block`: symmetric. `corner_inverse`: lower triangular, diagonal between 1 and 2.
All inputs are finite; a program needn't handle non-finite values.
Results may differ from a plain program's by a relative error of at most 0.00012.
Values sent between devices are 32-bit elements; how exact they have to be, the bound alone decides.
A program may use at most 192 MiB of HBM per device.

v0:
```python
import jax
import jax.numpy as jnp
from jax import lax
from jax.sharding import PartitionSpec as P


def broadcast(value, axis, source):
    kept = jnp.where(lax.axis_index(axis) == source, value, 0).astype(value.dtype)
    return lax.psum(kept, axis)


def matmul(left, right):
    return jnp.dot(left, right, precision=lax.Precision.HIGHEST, preferred_element_type=jnp.float32)


def contract(left, right):
    return lax.dot_general(
        left,
        right,
        (((1,), (1,)), ((), ())),
        precision=lax.Precision.HIGHEST,
        preferred_element_type=jnp.float32,
    )


def body(trailing, panel_block, factor_panel, corner_block, corner_inverse):
    row_count = panel_block.shape[0]
    stacked = jnp.concatenate([panel_block, corner_block], axis=0)
    product = contract(
        stacked, lax.all_gather(corner_inverse, ("row", "col", "depth"), axis=0, tiled=True)
    )
    scaled = product[:row_count]
    right_part = product[row_count:]
    columns = corner_inverse
    corner_out = matmul(
        columns, lax.all_gather(right_part, ("row", "col", "depth"), axis=0, tiled=True)
    )
    columns = factor_panel
    coupling = matmul(
        columns, lax.all_gather(corner_out, ("row", "col", "depth"), axis=0, tiled=True)
    )
    half_panel = scaled - 0.5 * coupling
    panel_out = half_panel - 0.5 * coupling
    half_cols, lower_cols = (
        lax.all_gather(half_panel, "depth", axis=0, tiled=True),
        lax.all_gather(factor_panel, "depth", axis=0, tiled=True),
    )
    half_piece = broadcast(half_panel, ("row", "col"), 0)
    lower_piece = broadcast(factor_panel, ("row", "col"), 0)
    update = contract(half_piece, lower_cols) + contract(lower_piece, half_cols)
    trailing_out = trailing - update
    return (trailing_out, panel_out, corner_out)


def solution(mesh):
    in_specs = (
        P("depth", ("row", "col")),
        P(("row", "col", "depth"), None),
        P(("row", "col", "depth"), None),
        P(("row", "col", "depth"), None),
        P(("row", "col", "depth"), None),
    )
    out_specs = (
        P("depth", ("row", "col")),
        P(("row", "col", "depth"), None),
        P(("row", "col", "depth"), None),
    )
    return jax.shard_map(body, mesh=mesh, in_specs=in_specs, out_specs=out_specs, check_vma=False)
```

profile of v0, /device:TPU:0, one launch (start us, length us, event | category | flops | bytes accessed | tf_op | source)
XLA Modules:
  0.0 837.7 jit_solution(5062860278421330772)
XLA Ops:
  7.2 0.0 all-gather.6.cloned.1.call-start
  7.2 0.7 all-gather.6.cloned.1.call-update
  7.9 0.0 copy-start.1
  7.9 0.0 all-gather.8.cloned.1.call-start
  8.0 67.6 %all-gather.6.cloned.1.call-done = f32[1024,1024]{1,0:T(8,128)} async-done(((f32[32,1024]{1,0:T(8,128)}), f32[1024,1024]{1,0:T(8,128)}) %all-gather.6.cloned.1.call-update) | async-done | bytes 4194320 | tf_op jit(solution)/shard_map/all_gather | solution.py:30
  75.5 23.7 %fusion = f32[1536,1024]{1,0:T(8,128)S(1)} fusion(f32[1024,1024]{1,0:T(8,128)} %all-gather.6.cloned.1.call-done, f32[32,1024]{1,0:T(8,128)} %param.8, f32[1504,1024]{1,0:T(8,128)} %param.6), kind=kOutput, calls=%fused_computation.1 | convolution fusion | flops 19328925696 | bytes 16777216 | tf_op jit(solution)/shard_map/dot_general | solution.py:17
  99.2 0.0 copy-start
  99.2 2.7 copy-done
  101.9 0.7 slice.9
  102.6 0.0 all-gather.8.cloned.1.call-update
  102.6 0.0 all-gather.10.cloned.1.call-start
  102.6 60.6 %all-gather.8.cloned.1.call-done = f32[1024,1024]{1,0:T(8,128)} async-done(((f32[32,1024]{1,0:T(8,128)}), f32[1024,1024]{1,0:T(8,128)}) %all-gather.8.cloned.1.call-update) | async-done | bytes 4194320 | tf_op jit(solution)/shard_map/all_gather | solution.py:36
  163.2 0.0 copy-done.1
  163.2 5.4 convolution_bitcast_fusion
  168.6 0.0 all-gather.10.cloned.1.call-update
  168.6 0.0 all-gather.12.cloned.1.call-start
  168.7 0.5 all-gather.12.cloned.1.call-update
  169.2 0.2 all-reduce.3.cloned.1.call-start
  169.5 6.7 broadcast_select_fusion
  176.1 53.2 %all-gather.10.cloned.1.call-done = f32[1024,1024]{1,0:T(8,128)} async-done(((f32[32,1024]{1,0:T(8,128)}), f32[1024,1024]{1,0:T(8,128)}) %all-gather.10.cloned.1.call-update) | async-done | bytes 4194320 | tf_op jit(solution)/shard_map/all_gather | solution.py:40
  229.3 25.3 %bitcast_subtract_fusion = (f32[1504,1024]{1,0:T(8,128)}, f32[1504,1024]{1,0:T(8,128)}) fusion(f32[1536,1024]{1,0:T(8,128)} %copy-done, f32[1024,1024]{1,0:T(8,128)} %all-gather.10.cloned.1.call-done, f32[1504,1024]{1,0:T(8,128)} %param.7), kind=kOutput, calls=%fused_computation.6 | convolution fusion | flops 18929319936 | bytes 28835840 | tf_op jit(solution)/shard_map/dot_general | solution.py:13
  254.6 6.7 broadcast_select_fusion.1
  261.3 0.0 all-reduce.3.cloned.1.call-update
  261.4 0.0 all-gather.14.cloned.1.call-start
  261.4 0.5 all-gather.14.cloned.1.call-update
  261.9 117.2 %all-gather.12.cloned.1.call-done = f32[3008,1024]{1,0:T(8,128)} async-done(((f32[1504,1024]{1,0:T(8,128)}), f32[3008,1024]{1,0:T(8,128)}) %all-gather.12.cloned.1.call-update) | async-done | bytes 12320784 | tf_op jit(solution)/shard_map/all_gather | solution.py:46
  379.1 233.9 %all-reduce.3.cloned.1.call-done = (f32[1504,1024]{1,0:T(8,128)}, f32[1504,1024]{1,0:T(8,128)}) async-done(((f32[1504,1024]{1,0:T(8,128)}, f32[1504,1024]{1,0:T(8,128)}), (f32[1504,1024]{1,0:T(8,128)}, f32[1504,1024]{1,0:T(8,128)})) %all-reduce.3.cloned.1.call-update) | async-done | bytes 12320784 | tf_op jit(solution)/shard_map/psum | solution.py:9
  613.1 67.2 %fusion.5 = f32[1504,3008]{1,0:T(8,128)} fusion(f32[1504,1024]{1,0:T(8,128)} %get-tuple-element.3, f32[3008,1024]{1,0:T(8,128)} %all-gather.12.cloned.1.call-done), kind=kOutput, calls=%fused_computation.11 | convolution fusion | flops 55591305216 | bytes 36577280 | tf_op jit(solution)/shard_map/dot_general | solution.py:17
  680.3 83.6 %all-gather.14.cloned.1.call-done = f32[3008,1024]{1,0:T(8,128)} async-done(((f32[1504,1024]{1,0:T(8,128)}), f32[3008,1024]{1,0:T(8,128)}) %all-gather.14.cloned.1.call-update) | async-done | bytes 12320784 | tf_op jit(solution)/shard_map/all_gather | solution.py:45
  763.9 66.9 %add_subtract_fusion = f32[1504,3008]{1,0:T(8,128)} fusion(f32[1504,3008]{1,0:T(8,128)} %param.5, f32[1504,3008]{1,0:T(8,128)} %fusion.5, f32[1504,1024]{1,0:T(8,128)} %get-tuple-element.4, f32[3008,1024]{1,0:T(8,128)} %all-gather.14.cloned.1.call-done), kind=kOutput, calls=%fused_computation | convolution fusion | flops 55600353280 | bytes 72769536 | tf_op jit(solution)/shard_map/dot_general | solution.py:17
Async XLA Ops:
  7.2 68.4 %all-gather.6.cloned.1.call-start = ((), (), s32[]{:S(2)}) async-start(), calls=%async_computation | async-start | bytes 4325376 | tf_op jit(solution)/shard_map/all_gather | solution.py:30
  7.9 155.3 %copy-start.1 = (f32[32,1024]{1,0:T(8,128)S(1)}, f32[32,1024]{1,0:T(8,128)}, u32[]{:S(2)}) copy-start(f32[32,1024]{1,0:T(8,128)} %param.9) | copy-start | bytes 393220
  7.9 155.3 %all-gather.8.cloned.1.call-start = ((), (), s32[]{:S(2)}) async-start(), calls=%async_computation.1 | async-start | bytes 4325376 | tf_op jit(solution)/shard_map/all_gather | solution.py:36
  99.2 2.7 copy-start
  102.6 126.7 %all-gather.10.cloned.1.call-start = ((), (), s32[]{:S(2)}) async-start(), calls=%async_computation.2 | async-start | bytes 4325376 | tf_op jit(solution)/shard_map/all_gather | solution.py:40
  168.6 210.5 %all-gather.12.cloned.1.call-start = ((), (), s32[]{:S(2)}) async-start(), calls=%async_computation.3 | async-start | bytes 18481152 | tf_op jit(solution)/shard_map/all_gather | solution.py:46
  169.2 443.8 %all-reduce.3.cloned.1.call-start = ((), (), s32[]{:S(2)}) async-start(), calls=%async_computation.5 | async-start | bytes 24641536 | tf_op jit(solution)/shard_map/psum | solution.py:9
  261.4 502.6 %all-gather.14.cloned.1.call-start = ((), (), s32[]{:S(2)}) async-start(), calls=%async_computation.4 | async-start | bytes 18481152 | tf_op jit(solution)/shard_map/all_gather | solution.py:45
Sparse Core Ops, SparseCore 0:
  11.1 64.4 all-gather.5
  102.7 60.4 all-gather.7
  168.8 60.4 all-gather.9
  230.7 148.3 all-gather.11
  383.8 229.1 all-reduce.2
  614.5 149.4 all-gather.13
where the time goes:
time: 838 us
  waiting for transfers between devices  618 us (74%)
  matrix products  189 us (23%)
  between operations  14.1 us (2%)
  other arithmetic  13.4 us (2%)
    psum x1, waiting for transfers between devices, broadcast(): return lax.psum(kept, axis)  234 us
    dot_general x3, matrix products, contract(): lax.dot_general(left, right, (((1,), (1,)), ((), ())), precision=lax.Prec...  158 us
    all_gather x1, waiting for transfers between devices, body(): lax.all_gather(factor_panel, 'depth', axis=0, tiled=True)  117 us
    all_gather x1, waiting for transfers between devices, body(): lax.all_gather(half_panel, 'depth', axis=0, tiled=True)  83.6 us
    all_gather x1, waiting for transfers between devices, body(): lax.all_gather(corner_inverse, ('row', 'col', 'depth'), axis=0, tiled=True)  67.6 us
    all_gather x1, waiting for transfers between devices, body(): lax.all_gather(right_part, ('row', 'col', 'depth'), axis=0, tiled=True)  60.6 us
    all_gather x1, waiting for transfers between devices, body(): lax.all_gather(corner_out, ('row', 'col', 'depth'), axis=0, tiled=True)  53.2 us
    dot_general x2, matrix products, matmul(): jnp.dot(left, right, precision=lax.Precision.HIGHEST, preferred_element_t...  30.7 us
  transfers between devices with their start and end apart: 6, of which 6 were waited for; matrix products, arithmetic and copies ran while one was open for 13% of the time, Pallas kernels for 0%

commit v1 on v0

v1 whole, which is shorter than its diff:
```python
import jax
import jax.numpy as jnp
from jax import lax
from jax.sharding import PartitionSpec as P

EVERY = ("row", "col", "depth")
PIECES = 1


def matmul(left, right):
    return jnp.dot(left, right, precision=lax.Precision.HIGH, preferred_element_type=jnp.float32)


def contract(left, right):
    return lax.dot_general(
        left,
        right,
        (((1,), (1,)), ((), ())),
        precision=lax.Precision.HIGH,
        preferred_element_type=jnp.float32,
    )


def after(value, earlier):
    return lax.optimization_barrier((value, earlier))[0]


def gather_corner(corner_block, corner_inverse):
    rows, width = corner_inverse.shape
    first = lax.axis_index(EVERY) * rows
    row = first + lax.broadcasted_iota(jnp.int32, (rows, width), 0)
    col = lax.broadcasted_iota(jnp.int32, (rows, width), 1)
    both = jnp.where(col > row, corner_block, corner_inverse)
    diagonal = jnp.sum(jnp.where(col == row, corner_block, 0.0), axis=1, keepdims=True)
    packed = jnp.concatenate([both, jnp.broadcast_to(diagonal, (rows, 128))], axis=1)
    return lax.all_gather(packed, EVERY, axis=0, tiled=True)


def unpack_corner(packed, width):
    row = lax.broadcasted_iota(jnp.int32, (width, width), 0)
    col = lax.broadcasted_iota(jnp.int32, (width, width), 1)
    both = packed[:, :width]
    inverse = jnp.where(col <= row, both, 0.0)
    upper = jnp.where(col > row, both, jnp.where(col == row, 0.5 * packed[:, width:width + 1], 0.0))
    return inverse, upper


def transform(panel, factor, inverse, corner):
    coupling = matmul(factor, corner)
    half = contract(panel, inverse) - 0.5 * coupling
    return half - 0.5 * coupling


def exchange(value, layers):
    blocks = [value]
    for shift in range(1, layers):
        pairs = [(source, (source + shift) % layers) for source in range(layers)]
        blocks.append(lax.ppermute(value, "depth", pairs))
    return blocks


def arrange(blocks, layers):
    if layers == 1:
        return blocks[0]
    me = lax.axis_index("depth")
    rows, width = blocks[0].shape
    whole = jnp.zeros((layers * rows, width), blocks[0].dtype)
    for shift, block in enumerate(blocks):
        place = lax.rem(me - shift + layers, layers)
        whole = lax.dynamic_update_slice(whole, block, (place * rows, 0))
    return whole


def make_body(layers):
    def body(trailing, panel_block, factor_panel, corner_block, corner_inverse):
        rows, width = panel_block.shape
        factor_blocks = exchange(factor_panel, layers)
        panel_blocks = exchange(panel_block, layers)
        packed = gather_corner(corner_block, corner_inverse)

        count = PIECES if rows % PIECES == 0 else 1
        size = rows // count
        source = lax.axis_index(("row", "col")) == 0
        slabs = []
        for piece in range(count):
            part = slice(piece * size, (piece + 1) * size)
            pair = (panel_block[part], factor_panel[part])
            if piece:
                pair = after(pair, slabs[-1])
            kept = jnp.where(source, jnp.concatenate(pair, axis=0), 0.0)
            slabs.append(lax.psum(kept, ("row", "col")))

        inverse, upper = unpack_corner(packed, width)
        triangle = matmul(inverse, contract(upper, inverse))
        corner = triangle + triangle.T
        corner_rows = corner_inverse.shape[0]
        corner_out = lax.dynamic_slice(
            corner, (lax.axis_index(EVERY) * corner_rows, 0), (corner_rows, width)
        )
        panel_out = transform(panel_block, factor_panel, inverse, corner)

        factor_cols = arrange(factor_blocks, layers)
        panel_cols = arrange(panel_blocks, layers)
        outs = []
        for piece in range(count):
            panel_piece, factor_piece = slabs[piece][:size], slabs[piece][size:]
            left = transform(panel_piece, factor_piece, inverse, corner)
            right = matmul(factor_piece, inverse)
            part = trailing[piece * size:(piece + 1) * size]
            outs.append((part - contract(left, factor_cols)) - contract(right, panel_cols))
        trailing_out = jnp.concatenate(outs, axis=0)
        return (trailing_out, panel_out, corner_out)

    return body


def solution(mesh):
    in_specs = (
        P("depth", ("row", "col")),
        P(EVERY, None),
        P(EVERY, None),
        P(EVERY, None),
        P(EVERY, None),
    )
    out_specs = (
        P("depth", ("row", "col")),
        P(EVERY, None),
        P(EVERY, None),
    )
    body = make_body(mesh.shape["depth"])
    return jax.shard_map(body, mesh=mesh, in_specs=in_specs, out_specs=out_specs, check_vma=False)
```

time: 838 us -> 482 us (0.58)
  waiting for transfers between devices: 618 us -> 235 us
  local copies, waits for them, and re-layouts: 3.37 us -> 41.7 us
  matrix products: 189 us -> 160 us
    all_gather x5 -> x1, waiting for transfers between devices: 382 us -> 0.01 us  [gather_corner(): return lax.all_gather(packed, EVERY, axis=0, tiled=True)]
    ppermute x0 -> x2, waiting for transfers between devices: none -> 235 us  [exchange(): blocks.append(lax.ppermute(value, 'depth', pairs))]
    psum x1, waiting for transfers between devices: 234 us -> 0.01 us  [body(): slabs.append(lax.psum(kept, ('row', 'col')))]
    dot_general x3 -> x5, matrix products: 158 us -> 115 us  [contract(): lax.dot_general(left, right, (((1,), (1,)), ((), ())), precision=lax.Prec...]
    dynamic_update_slice x0 -> x4, local copies, waits for them, and re-layouts: none -> 23.4 us  [arrange(): whole = lax.dynamic_update_slice(whole, block, (place * rows, 0))]
    dot_general x2 -> x4, matrix products: 30.7 us -> 45.3 us  [matmul(): jnp.dot(left, right, precision=lax.Precision.HIGH, preferred_element_type...]
    broadcast_in_dim x0 -> x3, local copies, waits for them, and re-layouts: none -> 12 us  [the longest x2 12 us: body(): kept = jnp.where(source, jnp.concatenate(pair, axis=0), 0.0)]
  transfers between devices with their start and end apart: 6 -> 4, of which waited for: 6 -> 2; matrix products, arithmetic and copies ran while one was open for 13% -> 22% of each run, Pallas kernels for 0% -> 0%
where the time goes in v1:
time: 482 us; the launch traced here: 477 us
  waiting for transfers between devices  235 us (49%)
  matrix products  160 us (33%)
  local copies, waits for them, and re-layouts  41.7 us (9%)
  other arithmetic  20.4 us (4%)
  between operations  16.1 us (3%)
    ppermute x2, waiting for transfers between devices, exchange(): blocks.append(lax.ppermute(value, 'depth', pairs))  235 us
    dot_general x5, matrix products, contract(): lax.dot_general(left, right, (((1,), (1,)), ((), ())), precision=lax.Prec...  115 us
    dot_general x4, matrix products, matmul(): jnp.dot(left, right, precision=lax.Precision.HIGH, preferred_element_type...  45.3 us
    dynamic_update_slice x4, local copies, waits for them, and re-layouts, arrange(): whole = lax.dynamic_update_slice(whole, block, (place * rows, 0))  23.4 us
    select_n x1, other arithmetic, body(): kept = jnp.where(source, jnp.concatenate(pair, axis=0), 0.0)  12.1 us
    broadcast_in_dim x2, local copies, waits for them, and re-layouts, body(): kept = jnp.where(source, jnp.concatenate(pair, axis=0), 0.0)  12 us
  transfers between devices with their start and end apart: 4, of which 2 were waited for; matrix products, arithmetic and copies ran while one was open for 22% of the time, Pallas kernels for 0%

profile of v1, /device:TPU:0, one launch (start us, length us, event | category | flops | bytes accessed | tf_op | source)
XLA Modules:
  0.0 476.8 jit_solution(9041454763933964617)
XLA Ops:
  8.0 0.0 all-gather.2.cloned.1.call-start
  8.1 1.2 fusion.32
  9.2 0.1 broadcast_in_dim.32
  9.3 0.7 pad_maximum_fusion
  10.0 0.0 all-gather.2.cloned.1.call-update
  10.0 0.0 all-reduce.2.cloned.1.call-start
  10.1 3.1 collective-permute-start
  13.1 0.1 collective-permute-start.1
  13.2 12.1 %maximum_select_fusion = f32[3008,1024]{1,0:T(8,128)} fusion(f32[1504,1024]{1,0:T(8,128)} %param.7, f32[1504,1024]{1,0:T(8,128)} %param.6, pred[]{:T(512)S(6)} %eq.9), kind=kLoop, calls=%fused_computation.1 | loop fusion | flops 6160384 | bytes 24641536 | tf_op jit(solution)/shard_map/jit(_where)/select_n | solution.py:90
  25.4 0.0 all-reduce.2.cloned.1.call-update
  25.4 6.0 %broadcast_in_dim.30.clone = f32[3008,1024]{1,0:T(8,128)} broadcast(f32[]{:T(128)} %constant.11.clone.1), dimensions={} | broadcast | bytes 12320772 | tf_op jit(solution)/shard_map/jit(_where)/broadcast_in_dim | solution.py:90
  31.4 0.0 slice-start
  31.4 7.3 %constant_dynamic-update-slice_fusion.3 = f32[3008,1024]{1,0:T(8,128)} fusion(f32[3008,1024]{1,0:T(8,128)} %broadcast_in_dim.30.clone, f32[1504,1024]{1,0:T(8,128)} %param.7, s32[]{:T(128)S(6)} %select_n.46), kind=kLoop, calls=%fused_computation.45 | loop fusion | bytes 12320772 | tf_op jit(solution)/shard_map/dynamic_update_slice | solution.py:70
  38.7 0.0 slice-start.1
  38.7 6.0 %broadcast_in_dim.30.clone.1 = f32[3008,1024]{1,0:T(8,128)} broadcast(f32[]{:T(128)} %constant.11.clone.1), dimensions={} | broadcast | bytes 12320772 | tf_op jit(solution)/shard_map/jit(_where)/broadcast_in_dim | solution.py:90
  44.7 0.0 slice-done
  44.7 0.0 slice-done.1
  44.7 3.2 constant_dynamic-update-slice_fusion.1
  47.9 110.7 %collective-permute-done = f32[1504,1024]{1,0:T(8,128)} collective-permute-done((f32[1504,1024]{1,0:T(8,128)}, f32[1504,1024]{1,0:T(8,128)}, u32[]{:S(2)}, u32[]{:S(2)}) %collective-permute-start) | collective-permute-done | bytes 6160416 | tf_op jit(solution)/shard_map/ppermute | solution.py:58
  158.6 6.4 %constant_dynamic-update-slice_fusion.2 = f32[3008,1024]{1,0:T(8,128)} fusion(f32[3008,1024]{1,0:T(8,128)} %constant_dynamic-update-slice_fusion.3, f32[1504,1024]{1,0:T(8,128)} %collective-permute-done, s32[]{:T(128)S(6)} %select_n.47), kind=kLoop, calls=%fused_computation.44 | loop fusion | bytes 12320772 | tf_op jit(solution)/shard_map/dynamic_update_slice | solution.py:70
  165.0 124.7 %collective-permute-done.1 = f32[1504,1024]{1,0:T(8,128)} collective-permute-done((f32[1504,1024]{1,0:T(8,128)}, f32[1504,1024]{1,0:T(8,128)}, u32[]{:S(2)}, u32[]{:S(2)}) %collective-permute-start.1) | collective-permute-done | bytes 6160416 | tf_op jit(solution)/shard_map/ppermute | solution.py:58
  289.8 6.4 %constant_dynamic-update-slice_fusion = f32[3008,1024]{1,0:T(8,128)} fusion(f32[3008,1024]{1,0:T(8,128)} %constant_dynamic-update-slice_fusion.1, f32[1504,1024]{1,0:T(8,128)} %collective-permute-done.1, s32[]{:T(128)S(6)} %select_n.47), kind=kLoop, calls=%fused_computation.42 | loop fusion | bytes 12320772 | tf_op jit(solution)/shard_map/dynamic_update_slice | solution.py:70
  296.2 0.0 all-gather.2.cloned.1.call-done
  296.2 0.0 slice-start.6
  296.2 1.4 fusion.31
  297.6 0.0 slice-start.7
  297.6 10.8 %fusion.8 = f32[1024,1024]{1,0:T(8,128)S(1)} fusion(f32[1024,1152]{1,0:T(8,128)} %all-gather.2.cloned.1.call-done, f32[1024]{0:T(1024)S(1)} %fusion.31), kind=kOutput, calls=%fused_computation.13 | convolution fusion | flops 6448742400 | bytes 12587008 | tf_op jit(solution)/shard_map/dot_general | solution.py:15
  308.4 0.0 slice-done.6
  308.4 0.0 slice-done.7
  308.4 8.2 %fusion.15 = f32[1024,1024]{1,0:T(8,128)} fusion(f32[1024,1024]{1,0:T(8,128)S(1)} %fusion.8, f32[1024,1152]{1,0:T(8,128)S(1)} %bitcast.21), kind=kOutput, calls=%fused_computation.21 | convolution fusion | flops 6444548096 | bytes 12582912 | tf_op jit(solution)/shard_map/dot_general | solution.py:11
  316.7 0.0 slice-start.2
  316.7 5.5 %copy.9 = f32[1024,1024]{0,1:T(8,128)} copy(f32[1024,1024]{1,0:T(8,128)} %fusion.15) | data formatting | bytes 8388608 | tf_op jit(solution)/shard_map/dot_general | solution.py:11
  322.1 0.0 slice-start.3
  322.1 0.0 slice-start.4
  322.1 5.0 %bitcast_add_fusion = f32[1024,1024]{1,0:T(8,128)S(1)} fusion(f32[1024,1024]{1,0:T(8,128)} %fusion.15, f32[1024,1024]{0,1:T(8,128)} %copy.9), kind=kLoop, calls=%fused_computation.12 | loop fusion | flops 1048576 | bytes 12582912 | tf_op jit(solution)/shard_map/add | solution.py:95
  327.1 0.0 copy-start
  327.1 0.7 constant_dynamic-slice_fusion
  327.8 0.0 slice-done.2
  327.9 0.0 slice-done.3
  327.9 0.0 slice-start.5
  327.9 15.0 %fusion.12 = f32[1024,1504]{0,1:T(8,128)S(1)} fusion(f32[1504,1024]{1,0:T(8,128)S(1)} %bitcast.17, f32[1024,1152]{1,0:T(8,128)} %all-gather.2.cloned.1.call-done), kind=kOutput, calls=%fused_computation.20 | convolution fusion | flops 9464446976 | bytes 16515072 | tf_op jit(solution)/shard_map/dot_general | solution.py:15
  342.8 0.0 copy-done
  342.9 0.0 slice-done.4
  342.9 0.0 slice-done.5
  342.9 11.7 %subtract_subtract_fusion.1 = f32[1504,1024]{1,0:T(8,128)} fusion(f32[1024,1504]{0,1:T(8,128)S(1)} %fusion.12, f32[1024,1024]{1,0:T(8,128)S(1)} %bitcast_add_fusion, f32[1504,1024]{1,0:T(8,128)S(1)} %bitcast.19), kind=kOutput, calls=%fused_computation.2 | convolution fusion | flops 9466970112 | bytes 22675456 | tf_op jit(solution)/shard_map/dot_general | solution.py:11
  354.6 0.0 all-reduce.2.cloned.1.call-done
  354.6 0.0 copy-start.1
  354.6 13.5 %fusion.6 = f32[1504,1024]{1,0:T(8,128)S(1)} fusion(f32[1024,1024]{1,0:T(8,128)} %copy-done, f32[3008,1024]{1,0:T(8,128)} %all-reduce.2.cloned.1.call-done), kind=kOutput, calls=%fused_computation.10 | convolution fusion | flops 9462349824 | bytes 16515072 | tf_op jit(solution)/shard_map/dot_general | solution.py:11
  368.1 0.0 copy-done.1
  368.1 0.0 slice-start.8
  368.1 13.6 %fusion.1 = f32[1504,1024]{1,0:T(8,128)} fusion(f32[3008,1024]{1,0:T(8,128)S(1)} %copy-done.1, f32[1024,1152]{1,0:T(8,128)} %all-gather.2.cloned.1.call-done), kind=kOutput, calls=%fused_computation.5 | convolution fusion | flops 9464446976 | bytes 16515072 | tf_op jit(solution)/shard_map/dot_general | solution.py:15
  381.7 0.0 slice-start.9
  381.7 37.4 %fusion = f32[1504,3008]{1,0:T(8,128)} fusion(f32[3008,1024]{1,0:T(8,128)} %constant_dynamic-update-slice_fusion.2, f32[1504,1024]{1,0:T(8,128)} %fusion.1, f32[1504,1024]{1,0:T(8,128)S(1)} %fusion.6), kind=kOutput, calls=%fused_computation.4 | convolution fusion | flops 27800272896 | bytes 42737664 | tf_op jit(solution)/shard_map/dot_general | solution.py:15
  419.1 0.0 slice-done.8
  419.1 0.0 slice-done.9
  419.1 11.9 %fusion.4 = f32[1504,1024]{1,0:T(8,128)S(1)} fusion(f32[3008,1024]{1,0:T(8,128)} %all-reduce.2.cloned.1.call-done, f32[1024,1152]{1,0:T(8,128)S(1)} %bitcast.23), kind=kOutput, calls=%fused_computation.8 | convolution fusion | flops 9464446976 | bytes 16515072 | tf_op jit(solution)/shard_map/dot_general | solution.py:11
  431.0 37.8 %subtract_subtract_fusion = f32[1504,3008]{1,0:T(8,128)} fusion(f32[1504,3008]{1,0:T(8,128)} %param.5, f32[1504,3008]{1,0:T(8,128)} %fusion, f32[1504,1024]{1,0:T(8,128)S(1)} %fusion.4, f32[3008,1024]{1,0:T(8,128)} %constant_dynamic-update-slice_fusion), kind=kOutput, calls=%fused_computation | convolution fusion | flops 27804700672 | bytes 72769536 | tf_op jit(solution)/shard_map/dot_general | solution.py:15
  (6 shorter events, 0.0 us)
Async XLA Ops:
  8.0 288.2 %all-gather.2.cloned.1.call-start = ((), (), s32[]{:S(2)}) async-start(), calls=%async_computation.1 | async-start | bytes 4866048 | tf_op jit(solution)/shard_map/all_gather | solution.py:36
  10.0 344.6 %all-reduce.2.cloned.1.call-start = ((), (), s32[]{:S(2)}) async-start(), calls=%async_computation | async-start | bytes 24641536 | tf_op jit(solution)/shard_map/psum | solution.py:91
  10.1 148.5 %collective-permute-start = (f32[1504,1024]{1,0:T(8,128)}, f32[1504,1024]{1,0:T(8,128)}, u32[]{:S(2)}, u32[]{:S(2)}) collective-permute-start(f32[1504,1024]{1,0:T(8,128)} %param.7), channel_id=1, source_target_pairs={{0,1},{1,0},{2,3},{3,2},{4,5},{5,4},{6,7},{7,6},{8,9},{9,8},{10,11... | collective-permute-start | bytes 18481160 | tf_op jit(solution)/shard_map/ppermute | solution.py:58
  13.1 276.6 %collective-permute-start.1 = (f32[1504,1024]{1,0:T(8,128)}, f32[1504,1024]{1,0:T(8,128)}, u32[]{:S(2)}, u32[]{:S(2)}) collective-permute-start(f32[1504,1024]{1,0:T(8,128)} %param.6), channel_id=1, source_target_pairs={{0,1},{1,0},{2,3},{3,2},{4,5},{5,4},{6,7},{7,6},{8,9},{9,8},{10,11... | collective-permute-start | bytes 18481160 | tf_op jit(solution)/shard_map/ppermute | solution.py:58
  31.4 13.4 %slice-start = ((s8[6160384]{0:T(1024)(128)(4,1)}), s8[4194304]{0:T(1024)(128)(4,1)S(1)}, s32[]{:S(2)}) async-start(s8[6160384]{0:T(1024)(128)(4,1)} %bitcast.14), calls=%async_computation.2 | async-start | bytes 8388608
  38.7 6.0 %slice-start.1 = ((s8[6160384]{0:T(1024)(128)(4,1)}), s8[1966080]{0:T(1024)(128)(4,1)S(1)}, s32[]{:S(2)}) async-start(s8[6160384]{0:T(1024)(128)(4,1)} %bitcast.14), calls=%async_computation.3 | async-start | bytes 3932160
  296.2 12.2 %slice-start.6 = ((s8[4718592]{0:T(1024)(128)(4,1)}), s8[4194304]{0:T(1024)(128)(4,1)S(1)}, s32[]{:S(2)}) async-start(s8[4718592]{0:T(1024)(128)(4,1)} %bitcast.20), calls=%async_computation.8 | async-start | bytes 8388608
  297.6 10.8 %slice-start.7 = ((s8[4718592]{0:T(1024)(128)(4,1)}), s8[524288]{0:T(1024)(128)(4,1)S(1)}, s32[]{:S(2)}) async-start(s8[4718592]{0:T(1024)(128)(4,1)} %bitcast.20), calls=%async_computation.9 | async-start | bytes 1048576
  316.7 11.2 %slice-start.2 = ((s8[6160384]{0:T(1024)(128)(4,1)}), s8[1966080]{0:T(1024)(128)(4,1)S(1)}, s32[]{:S(2)}) async-start(s8[6160384]{0:T(1024)(128)(4,1)} %bitcast.16), calls=%async_computation.4 | async-start | bytes 3932160
  322.1 5.7 %slice-start.3 = ((s8[6160384]{0:T(1024)(128)(4,1)}), s8[4194304]{0:T(1024)(128)(4,1)S(1)}, s32[]{:S(2)}) async-start(s8[6160384]{0:T(1024)(128)(4,1)} %bitcast.16), calls=%async_computation.5 | async-start | bytes 8388608
  322.1 20.7 %slice-start.4 = ((s8[6160384]{0:T(1024)(128)(4,1)}), s8[4194304]{0:T(1024)(128)(4,1)S(1)}, s32[]{:S(2)}) async-start(s8[6160384]{0:T(1024)(128)(4,1)} %bitcast.18), calls=%async_computation.6 | async-start | bytes 8388608
  327.1 15.7 %copy-start = (f32[1024,1024]{1,0:T(8,128)}, f32[1024,1024]{1,0:T(8,128)S(1)}, u32[]{:S(2)}) copy-start(f32[1024,1024]{1,0:T(8,128)S(1)} %bitcast_add_fusion) | copy-start | bytes 12582916
  327.9 15.0 %slice-start.5 = ((s8[6160384]{0:T(1024)(128)(4,1)}), s8[1966080]{0:T(1024)(128)(4,1)S(1)}, s32[]{:S(2)}) async-start(s8[6160384]{0:T(1024)(128)(4,1)} %bitcast.18), calls=%async_computation.7 | async-start | bytes 3932160
  354.6 13.5 %copy-start.1 = (f32[3008,1024]{1,0:T(8,128)S(1)}, f32[3008,1024]{1,0:T(8,128)}, u32[]{:S(2)}) copy-start(f32[3008,1024]{1,0:T(8,128)} %all-reduce.2.cloned.1.call-done) | copy-start | bytes 36962308
  368.1 51.0 %slice-start.8 = ((s8[4718592]{0:T(1024)(128)(4,1)}), s8[4194304]{0:T(1024)(128)(4,1)S(1)}, s32[]{:S(2)}) async-start(s8[4718592]{0:T(1024)(128)(4,1)} %bitcast.22), calls=%async_computation.10 | async-start | bytes 8388608
  381.7 37.4 %slice-start.9 = ((s8[4718592]{0:T(1024)(128)(4,1)}), s8[524288]{0:T(1024)(128)(4,1)S(1)}, s32[]{:S(2)}) async-start(s8[4718592]{0:T(1024)(128)(4,1)} %bitcast.22), calls=%async_computation.11 | async-start | bytes 1048576
Sparse Core Ops, SparseCore 0:
  12.3 97.3 all-gather.1
Sparse Core Ops, SparseCore 1:
  25.5 249.3 all-reduce.1
